TPU v7x, 128 devices: a whole 4x4x4 slice. The times are simulated.
128 devices in a mesh: seq: 64 (over z, y, x), tp: 2 (over core).
Axes of the slice: x: 4, y: 4, z: 4, core: 2. Of those that a mesh axis runs over, the one named last changes fastest.
Arguments:
- patches: bfloat16 [16384, 1280], P('seq'), may hold values from -60 to 60
- merge_up: bfloat16 [5120, 2560], P(None, 'tp'), may hold values from -0.078125 to 0.078125
- merge_down: bfloat16 [2560, 3584], P('tp'), may hold values from -0.125 to 0.125
- dest: int32 [4096], P('seq'), may hold values from 0 to 63, as said below
- slot: int32 [4096], P('seq'), may hold values from 0 to 255, as said below
- text: bfloat16 [16384, 3584], P('seq'), may hold values from -60 to 60
- positions: int32 [3, 16384], P(None, 'seq'), may hold values from 0 to 1023
- documents: int32 [16384], P('seq'), may hold values from 0 to 7, never falling along the last dimension, each value on 1 to 8448 neighbouring positions
- w_query: bfloat16 [3584, 1792], P('seq', 'tp'), may hold values from -8 to 8
- w_key: bfloat16 [3584, 256], P('seq', 'tp'), may hold values from -8 to 8
- w_value: bfloat16 [3584, 256], P('seq', 'tp'), may hold values from -0.09375 to 0.09375
Outputs:
- layer_input: bfloat16 [16384, 3584], P('seq', 'tp')
- attended: bfloat16 [16384, 1792], P('seq', 'tp')
Inputs may be any that keep to these rules, and one draw needn't show every extreme that they name: `dest`: the rows of one device name each sequence shard at most 2 times, and in every draw some sequence shard is named 2 times by the rows of every device. `slot`: no two image rows share both a sequence shard and a position. `documents`: document numbers never fall along the tokens.
All inputs are finite; a program needn't handle non-finite values.
Results may differ from a plain program's by a relative error of at most 0.0065.
Values may be sent and summed in bfloat16 or wider, within the bound.
A program may use at most 128 MiB of HBM per device.

v0:
```python
import jax
import jax.numpy as jnp
from jax import lax
from jax.sharding import PartitionSpec as P

HEAD = 128
epsilon = 1e-06
theta_base = 1000000.0
masked_score = -1e30
block_rows = 512


def copy_for_each(x, axis):
    size = lax.axis_size(axis)
    return lax.all_to_all(jnp.broadcast_to(x[None], (size, *x.shape)), axis, 0, 0, tiled=True)


def of_everyone(x, axis):
    everything = copy_for_each(x, axis)
    return jnp.sum(everything, axis=0)


def sent_together(arrays, axis, dim, along):
    ends, at = ([], 0)
    for a in arrays[:-1]:
        at += a.shape[along]
        ends.append(at)
    both = jnp.concatenate(arrays, axis=along)
    return tuple(jnp.split(lax.all_gather(both, axis, axis=dim, tiled=True), ends, axis=along))


def rms_rows(values):
    floats = values.astype(jnp.float32)
    return floats * lax.rsqrt(jnp.mean(floats * floats, axis=-1, keepdims=True) + epsilon)


def rotate(vectors, positions):
    half_dim = vectors.shape[-1] // 2
    first_end = half_dim // 4
    second_end = first_end + 3 * half_dim // 8
    pair_ids = jnp.arange(half_dim, dtype=jnp.int32)
    inverse = jnp.power(theta_base, -2.0 * pair_ids.astype(jnp.float32) / (2 * half_dim))
    coords = positions.astype(jnp.float32)
    chosen = jnp.where(
        pair_ids[None, :] < first_end,
        coords[0][:, None],
        jnp.where(pair_ids[None, :] < second_end, coords[1][:, None], coords[2][:, None]),
    )
    angles = chosen * inverse[None, :]
    cosine = jnp.cos(angles)[:, None, :]
    sine = jnp.sin(angles)[:, None, :]
    lower_part = vectors[..., :half_dim]
    upper_part = vectors[..., half_dim:]
    return jnp.concatenate(
        [lower_part * cosine - upper_part * sine, upper_part * cosine + lower_part * sine], axis=-1
    )


def attend(
    carry, queries, key_block, value_block, doc_block, key_first, query_pos, query_doc, score_scale
):
    maxima, totals, summed = carry
    scores = (
        jnp.einsum("qkgd,pkd->kgqp", queries, key_block, preferred_element_type=jnp.float32)
        * score_scale
    )
    key_pos = key_first + jnp.arange(key_block.shape[0], dtype=jnp.int32)
    allowed = (query_pos[:, None] >= key_pos[None, :]) & (query_doc[:, None] == doc_block[None, :])
    scores = jnp.where(allowed, scores, masked_score)
    new_max = jnp.maximum(maxima, jnp.max(scores, axis=-1))
    weights = jnp.where(allowed, jnp.exp(scores - new_max[..., None]), 0.0)
    factor = jnp.exp(maxima - new_max)
    totals = totals * factor + jnp.sum(weights, axis=-1)
    summed = summed * factor[..., None] + jnp.einsum(
        "kgqp,pkd->kgqd",
        weights.astype(jnp.bfloat16),
        value_block,
        preferred_element_type=jnp.float32,
    )
    return (new_max, totals, summed)


def per_device(
    patches, merge_up, merge_down, dest, slot, text, positions, documents, w_query, w_key, w_value
):
    seq_count = lax.axis_size("seq")
    tp_count = lax.axis_size("tp")
    tok_dev = text.shape[0]
    model_width = text.shape[1]
    img_dev = dest.shape[0]
    capacity = max(2, 2 * img_dev // seq_count)
    grouped = rms_rows(patches).astype(jnp.bfloat16).reshape(img_dev, -1)
    merger_hidden = jax.nn.gelu(
        jnp.dot(grouped, merge_up, preferred_element_type=jnp.float32), approximate=False
    ).astype(jnp.bfloat16)
    partial_sums = jnp.dot(merger_hidden, merge_down, preferred_element_type=jnp.float32)
    same_dest = dest[:, None] == dest[None, :]
    earlier = jnp.arange(img_dev)[:, None] > jnp.arange(img_dev)[None, :]
    slot_order = jnp.sum(same_dest & earlier, axis=1)
    send_place = dest * capacity + slot_order
    slot_buffer = jnp.full((seq_count * capacity,), tok_dev, jnp.int32).at[send_place].set(slot)
    slot_buffer = slot_buffer.reshape(seq_count, capacity)
    share_width = model_width // tp_count
    own_part = lax.axis_index("tp")
    merged = of_everyone(partial_sums, "tp").astype(jnp.bfloat16)
    buffer = jnp.zeros((seq_count * capacity, model_width), jnp.bfloat16).at[send_place].set(merged)
    buffer = buffer.reshape(seq_count, capacity, model_width)
    arrived, places = (
        lax.all_to_all(buffer, "seq", split_axis=0, concat_axis=0, tiled=True),
        lax.all_to_all(slot_buffer, "seq", split_axis=0, concat_axis=0, tiled=True),
    )
    layer_input = text.at[places.reshape(-1)].set(arrived.reshape(-1, model_width), mode="drop")
    layer_part = lax.dynamic_slice_in_dim(layer_input, own_part * share_width, share_width, 1)
    normed = rms_rows(layer_input).astype(jnp.bfloat16)
    pieces = sent_together((w_query, w_key, w_value), "seq", 0, 1)
    query_raw = jnp.dot(normed, pieces[0], preferred_element_type=jnp.float32)
    key_raw = jnp.dot(normed, pieces[1], preferred_element_type=jnp.float32)
    value_raw = jnp.dot(normed, pieces[2], preferred_element_type=jnp.float32)
    kv_local = w_key.shape[1] // HEAD
    group_size = w_query.shape[1] // w_key.shape[1]
    roped_query = rotate(query_raw.reshape(tok_dev, -1, HEAD), positions).astype(jnp.bfloat16)
    roped_query = roped_query.reshape(tok_dev, kv_local, group_size, HEAD)
    roped_key = rotate(key_raw.reshape(tok_dev, kv_local, HEAD), positions).astype(jnp.bfloat16)
    values = value_raw.reshape(tok_dev, kv_local, HEAD).astype(jnp.bfloat16)
    own_index = lax.axis_index("seq")
    queries = roped_query
    query_pos = own_index * tok_dev + jnp.arange(tok_dev, dtype=jnp.int32)
    last_query = jnp.max(query_pos)
    first_doc = jnp.min(documents)
    score_scale = HEAD ** (-0.5)

    def visit(carry, key_block, value_block, doc_block, key_first):
        unused = (key_first > last_query) | (doc_block[-1] < first_doc)
        return lax.cond(
            unused,
            lambda current: current,
            lambda current: attend(
                current,
                queries,
                key_block,
                value_block,
                doc_block,
                key_first,
                query_pos,
                documents,
                score_scale,
            ),
            carry,
        )

    initial = (
        jnp.full((kv_local, group_size, tok_dev), masked_score, jnp.float32),
        jnp.zeros((kv_local, group_size, tok_dev), jnp.float32),
        jnp.zeros((kv_local, group_size, tok_dev, HEAD), jnp.float32),
    )
    key_piece = lax.all_gather(roped_key, "seq", axis=0, tiled=True)
    value_piece = lax.all_gather(values, "seq", axis=0, tiled=True)
    doc_piece = lax.all_gather(documents, "seq", axis=0, tiled=True)
    piece_rows = key_piece.shape[0]
    block_count = piece_rows // block_rows
    stacked = (
        key_piece.reshape(block_count, block_rows, kv_local, HEAD),
        value_piece.reshape(block_count, block_rows, kv_local, HEAD),
        doc_piece.reshape(block_count, block_rows),
        jnp.arange(block_count, dtype=jnp.int32),
    )

    def through(current, parts):
        return (visit(current, parts[0], parts[1], parts[2], parts[3] * block_rows), None)

    finished, ignored = lax.scan(through, initial, stacked)
    maxima, totals, summed = finished
    attended = (
        (summed / totals[..., None]).transpose(2, 0, 1, 3).reshape(tok_dev, -1).astype(jnp.bfloat16)
    )
    return (layer_part, attended)


def solution(mesh):
    in_specs = (
        P("seq", None),
        P(None, "tp"),
        P("tp", None),
        P("seq"),
        P("seq"),
        P("seq", None),
        P(None, "seq"),
        P("seq"),
        P("seq", "tp"),
        P("seq", "tp"),
        P("seq", "tp"),
    )
    out_specs = (P("seq", "tp"), P("seq", "tp"))
    return jax.shard_map(
        per_device, mesh=mesh, in_specs=in_specs, out_specs=out_specs, check_vma=False
    )
```

profile of v0, /device:TPU:80, one launch (start us, length us, event | category | flops | bytes accessed | tf_op | source)
XLA Modules:
  0.0 469.6 jit_solution(3593981710146801849)
XLA Ops:
  9.7 12.3 %fusion.50 = f32[64,3584]{1,0:T(8,128)S(1)} fusion(bf16[1280,3584]{1,0:T(8,128)(2,1)} %param.17, bf16[64,5120]{1,0:T(8,128)(2,1)S(1)} %reshape.556, bf16[5120,1280]{1,0:T(8,128)(2,1)} %param.16), kind=kOutput, calls=%fused_computation.75 | convolution fusion | flops 1431388160 | bytes 23855104 | tf_op jit(solution)/shard_map/dot_general | solution.py:96
  23.4 3.7 all-to-all-start.1
  29.8 10.5 %all-to-all-start = ((s32[64,1,2]{2,1,0:T(1,128)}), s32[64,1,2]{2,1,0:T(1,128)S(1)}, u32[]{:S(2)}, u32[]{:S(2)}) async-start(s32[64,1,2]{2,1,0:T(1,128)} %bitcast.14), calls=%async_computation | async-start | bytes 65536 | tf_op jit(solution)/shard_map/all_to_all | solution.py:110
  41.5 2.3 scatter_custom_fusion.1
  46.4 9.1 %all-to-all-start.2 = ((bf16[64,2,3584]{2,1,0:T(2,128)(2,1)}), bf16[64,2,3584]{2,1,0:T(2,128)(2,1)S(1)}, u32[]{:S(2)}, u32[]{:S(2)}) async-start(bf16[64,2,3584]{2,1,0:T(2,128)(2,1)} %reshape.557), calls=%async_computation.2 | async-start | bytes 1835008 | tf_op jit(solution)/shard_map/all_to_all | solution.py:109
  56.8 11.5 %all-to-all-done.2 = bf16[64,2,3584]{2,1,0:T(2,128)(2,1)S(1)} async-done(((bf16[64,2,3584]{2,1,0:T(2,128)(2,1)}), bf16[64,2,3584]{2,1,0:T(2,128)(2,1)S(1)}, u32[]{:S(2)}, u32[]{:S(2)}) %all-to-all-start.2) | async-done | bytes 917536 | tf_op jit(solution)/shard_map/all_to_all | solution.py:109
  69.7 3.7 scatter_fusion
  73.8 16.7 %all-gather.6.cloned.1.call-done = bf16[3584,1152]{1,0:T(8,128)(2,1)} async-done(((bf16[56,1152]{1,0:T(8,128)(2,1)}), bf16[3584,1152]{1,0:T(8,128)(2,1)}) %all-gather.6.cloned.1.call-update) | async-done | bytes 8257552 | tf_op jit(solution)/shard_map/all_gather | solution.py:29
  90.5 2.0 convolution_bitcast_fusion
  93.6 2.5 convolution_convert_fusion
  97.5 138.7 %all-gather.1 = s32[64,1,256]{2,1,0:T(1,128)S(1)} all-gather(s32[1,1,256]{2,1,0:T(1,128)S(1)} %bitcast.97), channel_id=1, replica_groups=mesh['seq'=64,'tp'=2] {'seq'}, dimensions={0}, use_global_device_ids=true | all-gather | bytes 66560 | tf_op jit(solution)/shard_map/all_gather | solution.py:158
  237.7 5.5 %fusion.27 = f32[256,896]{0,1:T(8,128)S(1)} fusion(bf16[3584,1152]{1,0:T(8,128)(2,1)} %all-gather.6.cloned.1.call-done, bf16[256,3584]{1,0:T(8,128)(2,1)S(1)} %scatter_fusion, f32[256]{0:T(256)S(1)} %add_rsqrt_fusion), kind=kOutput, calls=%fused_computation.33 | convolution fusion | flops 1646919680 | bytes 9176064 | tf_op jit(solution)/shard_map/dot_general | solution.py:116
  243.7 6.4 %copy.44 = bf16[16384,1,128]{2,0,1:T(8,128)(2,1)} copy(bf16[16384,1,128]{0,2,1:T(8,128)(2,1)} %all-gather.8.cloned.1.call-done) | data formatting | bytes 8388608
  250.2 211.5 %while.15 = (s32[]{:T(128)}, f32[1,7,256]{2,1,0:T(8,128)S(1)}, f32[1,7,256]{2,1,0:T(8,128)S(1)}, f32[1,7,256,128]{3,2,1,0:T(8,128)S(1)}, s32[32]{0:T(128)S(1)}, ...) while((s32[]{:T(128)}, f32[1,7,256]{2,1,0:T(8,128)S(1)}, ...), condition=%wide.region_14.15_spmd.clone, body=%wide.region_9.14_spmd.clone.sunk | while | flops 482547712 | bytes 14221707 | solution.py:171
  269.5 5.2 %conditional.3 = (f32[1,7,256]{2,1,0:T(8,128)S(1)}, f32[1,7,256]{2,1,0:T(8,128)S(1)}, f32[1,7,256,128]{3,2,1,0:T(8,128)S(1)}) conditional(s32[]{:T(128)} %convert_element_type.127, (s32[]{:T(128)}, s32[]{:T(128)}, s32[256]{0:T(256)S(1)}, s32[1,512]{1,0:T(1,128)S(1)}, bf16[32,512,1,128]{3,1,2,0:T(8,128)(2,1)}, /*index=5*/s32[]{:T(128)}, ...), branch_computations={%region_10.12_spmd, %region_13.13_spmd} | conditional | flops 482547712 | bytes 14201888 | solution.py:134
  271.4 2.3 fusion.12
  278.6 5.2 %conditional.3 = (f32[1,7,256]{2,1,0:T(8,128)S(1)}, f32[1,7,256]{2,1,0:T(8,128)S(1)}, f32[1,7,256,128]{3,2,1,0:T(8,128)S(1)}) conditional(s32[]{:T(128)} %convert_element_type.127, (s32[]{:T(128)}, s32[]{:T(128)}, s32[256]{0:T(256)S(1)}, s32[1,512]{1,0:T(1,128)S(1)}, bf16[32,512,1,128]{3,1,2,0:T(8,128)(2,1)}, /*index=5*/s32[]{:T(128)}, ...), branch_computations={%region_10.12_spmd, %region_13.13_spmd} | conditional | flops 482547712 | bytes 14201888 | solution.py:134
  280.4 2.3 fusion.12
  287.6 5.2 %conditional.3 = (f32[1,7,256]{2,1,0:T(8,128)S(1)}, f32[1,7,256]{2,1,0:T(8,128)S(1)}, f32[1,7,256,128]{3,2,1,0:T(8,128)S(1)}) conditional(s32[]{:T(128)} %convert_element_type.127, (s32[]{:T(128)}, s32[]{:T(128)}, s32[256]{0:T(256)S(1)}, s32[1,512]{1,0:T(1,128)S(1)}, bf16[32,512,1,128]{3,1,2,0:T(8,128)(2,1)}, /*index=5*/s32[]{:T(128)}, ...), branch_computations={%region_10.12_spmd, %region_13.13_spmd} | conditional | flops 482547712 | bytes 14201888 | solution.py:134
  289.5 2.3 fusion.12
  296.6 5.2 %conditional.3 = (f32[1,7,256]{2,1,0:T(8,128)S(1)}, f32[1,7,256]{2,1,0:T(8,128)S(1)}, f32[1,7,256,128]{3,2,1,0:T(8,128)S(1)}) conditional(s32[]{:T(128)} %convert_element_type.127, (s32[]{:T(128)}, s32[]{:T(128)}, s32[256]{0:T(256)S(1)}, s32[1,512]{1,0:T(1,128)S(1)}, bf16[32,512,1,128]{3,1,2,0:T(8,128)(2,1)}, /*index=5*/s32[]{:T(128)}, ...), branch_computations={%region_10.12_spmd, %region_13.13_spmd} | conditional | flops 482547712 | bytes 14201888 | solution.py:134
  298.5 2.3 fusion.12
  305.6 5.2 %conditional.3 = (f32[1,7,256]{2,1,0:T(8,128)S(1)}, f32[1,7,256]{2,1,0:T(8,128)S(1)}, f32[1,7,256,128]{3,2,1,0:T(8,128)S(1)}) conditional(s32[]{:T(128)} %convert_element_type.127, (s32[]{:T(128)}, s32[]{:T(128)}, s32[256]{0:T(256)S(1)}, s32[1,512]{1,0:T(1,128)S(1)}, bf16[32,512,1,128]{3,1,2,0:T(8,128)(2,1)}, /*index=5*/s32[]{:T(128)}, ...), branch_computations={%region_10.12_spmd, %region_13.13_spmd} | conditional | flops 482547712 | bytes 14201888 | solution.py:134
  307.5 2.3 fusion.12
  314.6 5.2 %conditional.3 = (f32[1,7,256]{2,1,0:T(8,128)S(1)}, f32[1,7,256]{2,1,0:T(8,128)S(1)}, f32[1,7,256,128]{3,2,1,0:T(8,128)S(1)}) conditional(s32[]{:T(128)} %convert_element_type.127, (s32[]{:T(128)}, s32[]{:T(128)}, s32[256]{0:T(256)S(1)}, s32[1,512]{1,0:T(1,128)S(1)}, bf16[32,512,1,128]{3,1,2,0:T(8,128)(2,1)}, /*index=5*/s32[]{:T(128)}, ...), branch_computations={%region_10.12_spmd, %region_13.13_spmd} | conditional | flops 482547712 | bytes 14201888 | solution.py:134
  316.5 2.3 fusion.12
  323.6 5.2 %conditional.3 = (f32[1,7,256]{2,1,0:T(8,128)S(1)}, f32[1,7,256]{2,1,0:T(8,128)S(1)}, f32[1,7,256,128]{3,2,1,0:T(8,128)S(1)}) conditional(s32[]{:T(128)} %convert_element_type.127, (s32[]{:T(128)}, s32[]{:T(128)}, s32[256]{0:T(256)S(1)}, s32[1,512]{1,0:T(1,128)S(1)}, bf16[32,512,1,128]{3,1,2,0:T(8,128)(2,1)}, /*index=5*/s32[]{:T(128)}, ...), branch_computations={%region_10.12_spmd, %region_13.13_spmd} | conditional | flops 482547712 | bytes 14201888 | solution.py:134
  325.5 2.3 fusion.12
  332.6 5.2 %conditional.3 = (f32[1,7,256]{2,1,0:T(8,128)S(1)}, f32[1,7,256]{2,1,0:T(8,128)S(1)}, f32[1,7,256,128]{3,2,1,0:T(8,128)S(1)}) conditional(s32[]{:T(128)} %convert_element_type.127, (s32[]{:T(128)}, s32[]{:T(128)}, s32[256]{0:T(256)S(1)}, s32[1,512]{1,0:T(1,128)S(1)}, bf16[32,512,1,128]{3,1,2,0:T(8,128)(2,1)}, /*index=5*/s32[]{:T(128)}, ...), branch_computations={%region_10.12_spmd, %region_13.13_spmd} | conditional | flops 482547712 | bytes 14201888 | solution.py:134
  334.5 2.3 fusion.12
  341.7 5.2 %conditional.3 = (f32[1,7,256]{2,1,0:T(8,128)S(1)}, f32[1,7,256]{2,1,0:T(8,128)S(1)}, f32[1,7,256,128]{3,2,1,0:T(8,128)S(1)}) conditional(s32[]{:T(128)} %convert_element_type.127, (s32[]{:T(128)}, s32[]{:T(128)}, s32[256]{0:T(256)S(1)}, s32[1,512]{1,0:T(1,128)S(1)}, bf16[32,512,1,128]{3,1,2,0:T(8,128)(2,1)}, /*index=5*/s32[]{:T(128)}, ...), branch_computations={%region_10.12_spmd, %region_13.13_spmd} | conditional | flops 482547712 | bytes 14201888 | solution.py:134
  343.6 2.3 fusion.12
  350.7 5.2 %conditional.3 = (f32[1,7,256]{2,1,0:T(8,128)S(1)}, f32[1,7,256]{2,1,0:T(8,128)S(1)}, f32[1,7,256,128]{3,2,1,0:T(8,128)S(1)}) conditional(s32[]{:T(128)} %convert_element_type.127, (s32[]{:T(128)}, s32[]{:T(128)}, s32[256]{0:T(256)S(1)}, s32[1,512]{1,0:T(1,128)S(1)}, bf16[32,512,1,128]{3,1,2,0:T(8,128)(2,1)}, /*index=5*/s32[]{:T(128)}, ...), branch_computations={%region_10.12_spmd, %region_13.13_spmd} | conditional | flops 482547712 | bytes 14201888 | solution.py:134
  352.6 2.3 fusion.12
  359.7 5.2 %conditional.3 = (f32[1,7,256]{2,1,0:T(8,128)S(1)}, f32[1,7,256]{2,1,0:T(8,128)S(1)}, f32[1,7,256,128]{3,2,1,0:T(8,128)S(1)}) conditional(s32[]{:T(128)} %convert_element_type.127, (s32[]{:T(128)}, s32[]{:T(128)}, s32[256]{0:T(256)S(1)}, s32[1,512]{1,0:T(1,128)S(1)}, bf16[32,512,1,128]{3,1,2,0:T(8,128)(2,1)}, /*index=5*/s32[]{:T(128)}, ...), branch_computations={%region_10.12_spmd, %region_13.13_spmd} | conditional | flops 482547712 | bytes 14201888 | solution.py:134
  361.6 2.3 fusion.12
  368.7 5.2 %conditional.3 = (f32[1,7,256]{2,1,0:T(8,128)S(1)}, f32[1,7,256]{2,1,0:T(8,128)S(1)}, f32[1,7,256,128]{3,2,1,0:T(8,128)S(1)}) conditional(s32[]{:T(128)} %convert_element_type.127, (s32[]{:T(128)}, s32[]{:T(128)}, s32[256]{0:T(256)S(1)}, s32[1,512]{1,0:T(1,128)S(1)}, bf16[32,512,1,128]{3,1,2,0:T(8,128)(2,1)}, /*index=5*/s32[]{:T(128)}, ...), branch_computations={%region_10.12_spmd, %region_13.13_spmd} | conditional | flops 482547712 | bytes 14201888 | solution.py:134
  370.6 2.3 fusion.12
  377.7 5.2 %conditional.3 = (f32[1,7,256]{2,1,0:T(8,128)S(1)}, f32[1,7,256]{2,1,0:T(8,128)S(1)}, f32[1,7,256,128]{3,2,1,0:T(8,128)S(1)}) conditional(s32[]{:T(128)} %convert_element_type.127, (s32[]{:T(128)}, s32[]{:T(128)}, s32[256]{0:T(256)S(1)}, s32[1,512]{1,0:T(1,128)S(1)}, bf16[32,512,1,128]{3,1,2,0:T(8,128)(2,1)}, /*index=5*/s32[]{:T(128)}, ...), branch_computations={%region_10.12_spmd, %region_13.13_spmd} | conditional | flops 482547712 | bytes 14201888 | solution.py:134
  379.6 2.3 fusion.12
  386.7 5.2 %conditional.3 = (f32[1,7,256]{2,1,0:T(8,128)S(1)}, f32[1,7,256]{2,1,0:T(8,128)S(1)}, f32[1,7,256,128]{3,2,1,0:T(8,128)S(1)}) conditional(s32[]{:T(128)} %convert_element_type.127, (s32[]{:T(128)}, s32[]{:T(128)}, s32[256]{0:T(256)S(1)}, s32[1,512]{1,0:T(1,128)S(1)}, bf16[32,512,1,128]{3,1,2,0:T(8,128)(2,1)}, /*index=5*/s32[]{:T(128)}, ...), branch_computations={%region_10.12_spmd, %region_13.13_spmd} | conditional | flops 482547712 | bytes 14201888 | solution.py:134
  388.6 2.3 fusion.12
  395.7 5.2 %conditional.3 = (f32[1,7,256]{2,1,0:T(8,128)S(1)}, f32[1,7,256]{2,1,0:T(8,128)S(1)}, f32[1,7,256,128]{3,2,1,0:T(8,128)S(1)}) conditional(s32[]{:T(128)} %convert_element_type.127, (s32[]{:T(128)}, s32[]{:T(128)}, s32[256]{0:T(256)S(1)}, s32[1,512]{1,0:T(1,128)S(1)}, bf16[32,512,1,128]{3,1,2,0:T(8,128)(2,1)}, /*index=5*/s32[]{:T(128)}, ...), branch_computations={%region_10.12_spmd, %region_13.13_spmd} | conditional | flops 482547712 | bytes 14201888 | solution.py:134
  397.6 2.3 fusion.12
  404.8 5.2 %conditional.3 = (f32[1,7,256]{2,1,0:T(8,128)S(1)}, f32[1,7,256]{2,1,0:T(8,128)S(1)}, f32[1,7,256,128]{3,2,1,0:T(8,128)S(1)}) conditional(s32[]{:T(128)} %convert_element_type.127, (s32[]{:T(128)}, s32[]{:T(128)}, s32[256]{0:T(256)S(1)}, s32[1,512]{1,0:T(1,128)S(1)}, bf16[32,512,1,128]{3,1,2,0:T(8,128)(2,1)}, /*index=5*/s32[]{:T(128)}, ...), branch_computations={%region_10.12_spmd, %region_13.13_spmd} | conditional | flops 482547712 | bytes 14201888 | solution.py:134
  406.7 2.3 fusion.12
  413.8 5.2 %conditional.3 = (f32[1,7,256]{2,1,0:T(8,128)S(1)}, f32[1,7,256]{2,1,0:T(8,128)S(1)}, f32[1,7,256,128]{3,2,1,0:T(8,128)S(1)}) conditional(s32[]{:T(128)} %convert_element_type.127, (s32[]{:T(128)}, s32[]{:T(128)}, s32[256]{0:T(256)S(1)}, s32[1,512]{1,0:T(1,128)S(1)}, bf16[32,512,1,128]{3,1,2,0:T(8,128)(2,1)}, /*index=5*/s32[]{:T(128)}, ...), branch_computations={%region_10.12_spmd, %region_13.13_spmd} | conditional | flops 482547712 | bytes 14201888 | solution.py:134
  415.7 2.3 fusion.12
  (376 shorter events, 106.0 us)
Async XLA Ops:
  7.2 1.7 copy-start.1
  7.2 1.0 copy-start.2
  7.2 1.0 copy-start.5
  7.2 0.9 copy-start.4
  7.2 83.3 %all-gather.6.cloned.1.call-start = ((), (), s32[]{:S(2)}) async-start(), calls=%async_computation.3 | async-start | bytes 8386560 | tf_op jit(solution)/shard_map/all_gather | solution.py:29
  21.9 5.3 %copy-start.7 = (s32[64]{0:T(128)S(1)}, s32[64]{0:T(128)}, u32[]{:S(2)}) copy-start(s32[64]{0:T(128)} %param.18) | copy-start | bytes 772
  23.4 6.4 %all-to-all-start.1 = ((f32[2,64,3584]{2,1,0:T(8,128)}), f32[2,64,3584]{2,1,0:T(8,128)S(1)}, u32[]{:S(2)}, u32[]{:S(2)}) async-start(f32[2,64,3584]{2,1,0:T(8,128)} %broadcast_in_dim.137), calls=%async_computation.1 | async-start | bytes 3670016 | tf_op jit(solution)/shard_map/all_to_all | solution.py:15
  29.8 16.5 %all-to-all-start = ((s32[64,1,2]{2,1,0:T(1,128)}), s32[64,1,2]{2,1,0:T(1,128)S(1)}, u32[]{:S(2)}, u32[]{:S(2)}) async-start(s32[64,1,2]{2,1,0:T(1,128)} %bitcast.14), calls=%async_computation | async-start | bytes 65536 | tf_op jit(solution)/shard_map/all_to_all | solution.py:110
  40.4 15.1 %copy-start.6 = (s32[3,256]{1,0:T(4,128)S(1)}, s32[3,256]{1,0:T(4,128)}, u32[]{:S(2)}) copy-start(s32[3,256]{1,0:T(4,128)} %param.21) | copy-start | bytes 9220
  41.5 28.1 %copy-start = (bf16[256,3584]{1,0:T(8,128)(2,1)S(1)}, bf16[256,3584]{1,0:T(8,128)(2,1)}, u32[]{:S(2)}) copy-start(bf16[256,3584]{1,0:T(8,128)(2,1)} %param.20) | copy-start | bytes 5505028
  46.4 22.0 %all-to-all-start.2 = ((bf16[64,2,3584]{2,1,0:T(2,128)(2,1)}), bf16[64,2,3584]{2,1,0:T(2,128)(2,1)S(1)}, u32[]{:S(2)}, u32[]{:S(2)}) async-start(bf16[64,2,3584]{2,1,0:T(2,128)(2,1)} %reshape.557), calls=%async_computation.2 | async-start | bytes 1835008 | tf_op jit(solution)/shard_map/all_to_all | solution.py:109
  55.4 188.3 %all-gather.8.cloned.1.call-start = ((), (), s32[]{:S(2)}) async-start(), calls=%async_computation.4 | async-start | bytes 4259840 | tf_op jit(solution)/shard_map/all_gather | solution.py:156
  73.8 23.0 %copy-start.3 = (s32[256]{0:T(256)S(1)}, s32[256]{0:T(256)}, u32[]{:S(2)}) copy-start(s32[256]{0:T(256)} %param.22) | copy-start | bytes 3076
  93.5 156.6 %all-gather.10.cloned.1.call-start = ((), (), s32[]{:S(2)}) async-start(), calls=%async_computation.5 | async-start | bytes 4259840 | tf_op jit(solution)/shard_map/all_gather | solution.py:157
Sparse Core Ops, SparseCore 0:
  11.5 78.9 all-gather.5
  93.8 74.6 all-gather.7
  171.4 66.6 all-gather.9
where the time goes:
time: 472 us; the launch traced here: 470 us
  blocking collectives  139 us (29%)
  matrix products  89.6 us (19%)
  loops' own time  85.4 us (18%)
  local copies, waits for them, and re-layouts  60 us (13%)
  waiting for transfers between devices  30.4 us (6%)
  other arithmetic  28.1 us (6%)
  starting transfers between devices  23.4 us (5%)
  between operations  14.1 us (3%)
    all_gather x1, blocking collectives, per_device(): doc_piece = lax.all_gather(documents, 'seq', axis=0, tiled=True)  139 us
    another operation x1, loops' own time, per_device(): finished, ignored = lax.scan(through, initial, stacked)  83.7 us
    dot_general x17, matrix products, attend(): jnp.einsum('kgqp,pkd->kgqd', weights.astype(jnp.bfloat16), value_block, p...  39.7 us
    dot_general x17, matrix products, attend(): jnp.einsum('qkgd,pkd->kgqp', queries, key_block, preferred_element_type=j...  27.6 us
    dynamic_slice x64, local copies, waits for them, and re-layouts, per_device(): finished, ignored = lax.scan(through, initial, stacked)  20.2 us
    slice x32, local copies, waits for them, and re-layouts, visit(): unused = (key_first > last_query) | (doc_block[-1] < first_doc)  19.2 us
    all_gather x1, waiting for transfers between devices, sent_together(): lax.all_gather(both, axis, axis=dim, tiled=True)  16.7 us
    reduce_sum x17, other arithmetic, attend(): totals = totals * factor + jnp.sum(weights, axis=-1)  15.2 us
  transfers between devices with their start and end apart: 6, of which 4 were waited for; matrix products, arithmetic and copies ran while one was open for 10% of the time, Pallas kernels for 0%

commit v1 on v0

--- a/solution.py
+++ b/solution.py
@@ -155,7 +155,11 @@
     )
     key_piece = lax.all_gather(roped_key, "seq", axis=0, tiled=True)
     value_piece = lax.all_gather(values, "seq", axis=0, tiled=True)
-    doc_piece = lax.all_gather(documents, "seq", axis=0, tiled=True)
+    length = lax.axis_size("seq")
+    repeats = [length if d == 0 else 1 for d in range(documents.ndim)]
+    doc_piece = lax.all_to_all(
+        jnp.tile(documents, repeats), "seq", split_axis=0, concat_axis=0, tiled=True
+    )
     piece_rows = key_piece.shape[0]
     block_count = piece_rows // block_rows
     stacked = (

time: 472 us -> 462 us (0.979)
  blocking collectives: 139 us -> 0 us
  waiting for transfers between devices: 30.4 us -> 147 us
  starting transfers between devices: 23.4 us -> 32.9 us
    all_gather x1 -> x0, blocking collectives: 139 us -> none  [per_device(): doc_piece = lax.all_gather(documents, 'seq', axis=0, tiled=True)]
    all_gather x1, waiting for transfers between devices: 0.01 us -> 63.2 us  [per_device(): value_piece = lax.all_gather(values, 'seq', axis=0, tiled=True)]
    all_gather x1, waiting for transfers between devices: 0.02 us -> 48.9 us  [per_device(): key_piece = lax.all_gather(roped_key, 'seq', axis=0, tiled=True)]
    all_to_all x0 -> x1, starting transfers between devices: none -> 9.46 us  [per_device(): lax.all_to_all(jnp.tile(documents, repeats), 'seq', split_axis=0, concat_...]
  transfers between devices with their start and end apart: 6 -> 7, of which waited for: 4 -> 7; matrix products, arithmetic and copies ran while one was open for 10% -> 10% of each run, Pallas kernels for 0% -> 0%
where the time goes in v1:
time: 462 us; the launch traced here: 460 us
  waiting for transfers between devices  147 us (32%)
  matrix products  89.6 us (19%)
  loops' own time  85.1 us (18%)
  local copies, waits for them, and re-layouts  63 us (14%)
  starting transfers between devices  32.9 us (7%)
  other arithmetic  28.1 us (6%)
  between operations  14.1 us (3%)
    another operation x1, loops' own time, per_device(): finished, ignored = lax.scan(through, initial, stacked)  83.5 us
    all_gather x1, waiting for transfers between devices, per_device(): value_piece = lax.all_gather(values, 'seq', axis=0, tiled=True)  63.2 us
    all_gather x1, waiting for transfers between devices, per_device(): key_piece = lax.all_gather(roped_key, 'seq', axis=0, tiled=True)  48.9 us
    dot_general x17, matrix products, attend(): jnp.einsum('kgqp,pkd->kgqd', weights.astype(jnp.bfloat16), value_block, p...  39.7 us
    dot_general x17, matrix products, attend(): jnp.einsum('qkgd,pkd->kgqp', queries, key_block, preferred_element_type=j...  27.6 us
    dynamic_slice x64, local copies, waits for them, and re-layouts, per_device(): finished, ignored = lax.scan(through, initial, stacked)  21.8 us
    slice x32, local copies, waits for them, and re-layouts, visit(): unused = (key_first > last_query) | (doc_block[-1] < first_doc)  19.9 us
    all_gather x1, waiting for transfers between devices, sent_together(): lax.all_gather(both, axis, axis=dim, tiled=True)  16.7 us
  transfers between devices with their start and end apart: 7, of which 7 were waited for; matrix products, arithmetic and copies ran while one was open for 10% of the time, Pallas kernels for 0%

profile of v1, /device:TPU:80, one launch (start us, length us, event | category | flops | bytes accessed | tf_op | source)
XLA Modules:
  0.0 459.5 jit_solution(12012696142658947123)
XLA Ops:
  9.7 12.3 %fusion.50 = f32[64,3584]{1,0:T(8,128)S(1)} fusion(bf16[1280,3584]{1,0:T(8,128)(2,1)} %param.17, bf16[64,5120]{1,0:T(8,128)(2,1)S(1)} %reshape.561, bf16[5120,1280]{1,0:T(8,128)(2,1)} %param.16), kind=kOutput, calls=%fused_computation.75 | convolution fusion | flops 1431388160 | bytes 23855104 | tf_op jit(solution)/shard_map/dot_general | solution.py:96
  23.4 3.7 all-to-all-start.1
  29.8 10.5 %all-to-all-start = ((s32[64,1,2]{2,1,0:T(1,128)}), s32[64,1,2]{2,1,0:T(1,128)S(1)}, u32[]{:S(2)}, u32[]{:S(2)}) async-start(s32[64,1,2]{2,1,0:T(1,128)} %bitcast.14), calls=%async_computation | async-start | bytes 65536 | tf_op jit(solution)/shard_map/all_to_all | solution.py:110
  46.4 9.1 %all-to-all-start.2 = ((bf16[64,2,3584]{2,1,0:T(2,128)(2,1)}), bf16[64,2,3584]{2,1,0:T(2,128)(2,1)S(1)}, u32[]{:S(2)}, u32[]{:S(2)}) async-start(bf16[64,2,3584]{2,1,0:T(2,128)(2,1)} %reshape.562), calls=%async_computation.2 | async-start | bytes 1835008 | tf_op jit(solution)/shard_map/all_to_all | solution.py:109
  57.0 11.3 %all-to-all-done.2 = bf16[64,2,3584]{2,1,0:T(2,128)(2,1)S(1)} async-done(((bf16[64,2,3584]{2,1,0:T(2,128)(2,1)}), bf16[64,2,3584]{2,1,0:T(2,128)(2,1)S(1)}, u32[]{:S(2)}, u32[]{:S(2)}) %all-to-all-start.2) | async-done | bytes 917536 | tf_op jit(solution)/shard_map/all_to_all | solution.py:109
  69.7 3.7 scatter_fusion
  73.8 16.7 %all-gather.5.cloned.1.call-done = bf16[3584,1152]{1,0:T(8,128)(2,1)} async-done(((bf16[56,1152]{1,0:T(8,128)(2,1)}), bf16[3584,1152]{1,0:T(8,128)(2,1)}) %all-gather.5.cloned.1.call-update) | async-done | bytes 8257552 | tf_op jit(solution)/shard_map/all_gather | solution.py:29
  93.6 2.5 convolution_convert_fusion
  96.8 9.5 %all-to-all-start.3 = ((s32[64,256,1]{1,2,0:T(1,128)}), s32[64,256,1]{1,2,0:T(1,128)S(1)}, u32[]{:S(2)}, u32[]{:S(2)}) async-start(s32[64,256,1]{1,2,0:T(1,128)} %all_to_all.22), calls=%async_computation.3 | async-start | bytes 131072 | tf_op jit(solution)/shard_map/all_to_all | solution.py:160
  107.9 4.5 all-to-all-done.3
  113.5 5.5 %fusion.27 = f32[256,896]{0,1:T(8,128)S(1)} fusion(bf16[3584,1152]{1,0:T(8,128)(2,1)} %all-gather.5.cloned.1.call-done, bf16[256,3584]{1,0:T(8,128)(2,1)S(1)} %scatter_fusion, f32[256]{0:T(256)S(1)} %add_rsqrt_fusion), kind=kOutput, calls=%fused_computation.33 | convolution fusion | flops 1646919680 | bytes 9176064 | tf_op jit(solution)/shard_map/dot_general | solution.py:116
  119.5 48.9 %all-gather.7.cloned.1.call-done = bf16[16384,1,128]{0,2,1:T(8,128)(2,1)} async-done(((bf16[256,1,128]{0,2,1:T(8,128)(2,1)}), bf16[16384,1,128]{0,2,1:T(8,128)(2,1)}) %all-gather.7.cloned.1.call-update) | async-done | bytes 4194320 | tf_op jit(solution)/shard_map/all_gather | solution.py:156
  168.4 6.4 %copy.44 = bf16[16384,1,128]{2,0,1:T(8,128)(2,1)} copy(bf16[16384,1,128]{0,2,1:T(8,128)(2,1)} %all-gather.7.cloned.1.call-done) | data formatting | bytes 8388608
  174.7 63.2 %all-gather.9.cloned.1.call-done = bf16[16384,128]{1,0:T(8,128)(2,1)} async-done(((bf16[256,128]{1,0:T(8,128)(2,1)}), bf16[16384,128]{1,0:T(8,128)(2,1)}) %all-gather.9.cloned.1.call-update) | async-done | bytes 4194320 | tf_op jit(solution)/shard_map/all_gather | solution.py:157
  238.0 213.6 %while.15 = (s32[]{:T(128)}, f32[1,7,256]{2,1,0:T(8,128)S(1)}, f32[1,7,256]{2,1,0:T(8,128)S(1)}, f32[1,7,256,128]{3,2,1,0:T(8,128)S(1)}, s32[32]{0:T(128)S(1)}, ...) while((s32[]{:T(128)}, f32[1,7,256]{2,1,0:T(8,128)S(1)}, ...), condition=%wide.region_14.15_spmd.clone, body=%wide.region_9.14_spmd.clone.sunk | while | flops 482547712 | bytes 14221707 | solution.py:175
  257.7 5.2 %conditional.3 = (f32[1,7,256]{2,1,0:T(8,128)S(1)}, f32[1,7,256]{2,1,0:T(8,128)S(1)}, f32[1,7,256,128]{3,2,1,0:T(8,128)S(1)}) conditional(s32[]{:T(128)} %convert_element_type.127, (s32[]{:T(128)}, s32[]{:T(128)}, s32[256]{0:T(256)S(1)}, s32[1,512]{1,0:T(1,128)S(1)}, bf16[32,512,1,128]{3,1,2,0:T(8,128)(2,1)}, /*index=5*/s32[]{:T(128)}, ...), branch_computations={%region_10.12_spmd, %region_13.13_spmd} | conditional | flops 482547712 | bytes 14201888 | solution.py:134
  259.6 2.3 fusion.12
  266.8 5.2 %conditional.3 = (f32[1,7,256]{2,1,0:T(8,128)S(1)}, f32[1,7,256]{2,1,0:T(8,128)S(1)}, f32[1,7,256,128]{3,2,1,0:T(8,128)S(1)}) conditional(s32[]{:T(128)} %convert_element_type.127, (s32[]{:T(128)}, s32[]{:T(128)}, s32[256]{0:T(256)S(1)}, s32[1,512]{1,0:T(1,128)S(1)}, bf16[32,512,1,128]{3,1,2,0:T(8,128)(2,1)}, /*index=5*/s32[]{:T(128)}, ...), branch_computations={%region_10.12_spmd, %region_13.13_spmd} | conditional | flops 482547712 | bytes 14201888 | solution.py:134
  275.9 5.2 %conditional.3 = (f32[1,7,256]{2,1,0:T(8,128)S(1)}, f32[1,7,256]{2,1,0:T(8,128)S(1)}, f32[1,7,256,128]{3,2,1,0:T(8,128)S(1)}) conditional(s32[]{:T(128)} %convert_element_type.127, (s32[]{:T(128)}, s32[]{:T(128)}, s32[256]{0:T(256)S(1)}, s32[1,512]{1,0:T(1,128)S(1)}, bf16[32,512,1,128]{3,1,2,0:T(8,128)(2,1)}, /*index=5*/s32[]{:T(128)}, ...), branch_computations={%region_10.12_spmd, %region_13.13_spmd} | conditional | flops 482547712 | bytes 14201888 | solution.py:134
  277.8 2.3 fusion.12
  285.0 5.2 %conditional.3 = (f32[1,7,256]{2,1,0:T(8,128)S(1)}, f32[1,7,256]{2,1,0:T(8,128)S(1)}, f32[1,7,256,128]{3,2,1,0:T(8,128)S(1)}) conditional(s32[]{:T(128)} %convert_element_type.127, (s32[]{:T(128)}, s32[]{:T(128)}, s32[256]{0:T(256)S(1)}, s32[1,512]{1,0:T(1,128)S(1)}, bf16[32,512,1,128]{3,1,2,0:T(8,128)(2,1)}, /*index=5*/s32[]{:T(128)}, ...), branch_computations={%region_10.12_spmd, %region_13.13_spmd} | conditional | flops 482547712 | bytes 14201888 | solution.py:134
  286.9 2.3 fusion.12
  294.0 5.2 %conditional.3 = (f32[1,7,256]{2,1,0:T(8,128)S(1)}, f32[1,7,256]{2,1,0:T(8,128)S(1)}, f32[1,7,256,128]{3,2,1,0:T(8,128)S(1)}) conditional(s32[]{:T(128)} %convert_element_type.127, (s32[]{:T(128)}, s32[]{:T(128)}, s32[256]{0:T(256)S(1)}, s32[1,512]{1,0:T(1,128)S(1)}, bf16[32,512,1,128]{3,1,2,0:T(8,128)(2,1)}, /*index=5*/s32[]{:T(128)}, ...), branch_computations={%region_10.12_spmd, %region_13.13_spmd} | conditional | flops 482547712 | bytes 14201888 | solution.py:134
  295.9 2.3 fusion.12
  303.1 5.2 %conditional.3 = (f32[1,7,256]{2,1,0:T(8,128)S(1)}, f32[1,7,256]{2,1,0:T(8,128)S(1)}, f32[1,7,256,128]{3,2,1,0:T(8,128)S(1)}) conditional(s32[]{:T(128)} %convert_element_type.127, (s32[]{:T(128)}, s32[]{:T(128)}, s32[256]{0:T(256)S(1)}, s32[1,512]{1,0:T(1,128)S(1)}, bf16[32,512,1,128]{3,1,2,0:T(8,128)(2,1)}, /*index=5*/s32[]{:T(128)}, ...), branch_computations={%region_10.12_spmd, %region_13.13_spmd} | conditional | flops 482547712 | bytes 14201888 | solution.py:134
  305.0 2.3 fusion.12
  312.2 5.2 %conditional.3 = (f32[1,7,256]{2,1,0:T(8,128)S(1)}, f32[1,7,256]{2,1,0:T(8,128)S(1)}, f32[1,7,256,128]{3,2,1,0:T(8,128)S(1)}) conditional(s32[]{:T(128)} %convert_element_type.127, (s32[]{:T(128)}, s32[]{:T(128)}, s32[256]{0:T(256)S(1)}, s32[1,512]{1,0:T(1,128)S(1)}, bf16[32,512,1,128]{3,1,2,0:T(8,128)(2,1)}, /*index=5*/s32[]{:T(128)}, ...), branch_computations={%region_10.12_spmd, %region_13.13_spmd} | conditional | flops 482547712 | bytes 14201888 | solution.py:134
  314.1 2.3 fusion.12
  321.3 5.2 %conditional.3 = (f32[1,7,256]{2,1,0:T(8,128)S(1)}, f32[1,7,256]{2,1,0:T(8,128)S(1)}, f32[1,7,256,128]{3,2,1,0:T(8,128)S(1)}) conditional(s32[]{:T(128)} %convert_element_type.127, (s32[]{:T(128)}, s32[]{:T(128)}, s32[256]{0:T(256)S(1)}, s32[1,512]{1,0:T(1,128)S(1)}, bf16[32,512,1,128]{3,1,2,0:T(8,128)(2,1)}, /*index=5*/s32[]{:T(128)}, ...), branch_computations={%region_10.12_spmd, %region_13.13_spmd} | conditional | flops 482547712 | bytes 14201888 | solution.py:134
  323.2 2.3 fusion.12
  330.4 5.2 %conditional.3 = (f32[1,7,256]{2,1,0:T(8,128)S(1)}, f32[1,7,256]{2,1,0:T(8,128)S(1)}, f32[1,7,256,128]{3,2,1,0:T(8,128)S(1)}) conditional(s32[]{:T(128)} %convert_element_type.127, (s32[]{:T(128)}, s32[]{:T(128)}, s32[256]{0:T(256)S(1)}, s32[1,512]{1,0:T(1,128)S(1)}, bf16[32,512,1,128]{3,1,2,0:T(8,128)(2,1)}, /*index=5*/s32[]{:T(128)}, ...), branch_computations={%region_10.12_spmd, %region_13.13_spmd} | conditional | flops 482547712 | bytes 14201888 | solution.py:134
  332.3 2.3 fusion.12
  339.4 5.2 %conditional.3 = (f32[1,7,256]{2,1,0:T(8,128)S(1)}, f32[1,7,256]{2,1,0:T(8,128)S(1)}, f32[1,7,256,128]{3,2,1,0:T(8,128)S(1)}) conditional(s32[]{:T(128)} %convert_element_type.127, (s32[]{:T(128)}, s32[]{:T(128)}, s32[256]{0:T(256)S(1)}, s32[1,512]{1,0:T(1,128)S(1)}, bf16[32,512,1,128]{3,1,2,0:T(8,128)(2,1)}, /*index=5*/s32[]{:T(128)}, ...), branch_computations={%region_10.12_spmd, %region_13.13_spmd} | conditional | flops 482547712 | bytes 14201888 | solution.py:134
  341.3 2.3 fusion.12
  348.5 5.2 %conditional.3 = (f32[1,7,256]{2,1,0:T(8,128)S(1)}, f32[1,7,256]{2,1,0:T(8,128)S(1)}, f32[1,7,256,128]{3,2,1,0:T(8,128)S(1)}) conditional(s32[]{:T(128)} %convert_element_type.127, (s32[]{:T(128)}, s32[]{:T(128)}, s32[256]{0:T(256)S(1)}, s32[1,512]{1,0:T(1,128)S(1)}, bf16[32,512,1,128]{3,1,2,0:T(8,128)(2,1)}, /*index=5*/s32[]{:T(128)}, ...), branch_computations={%region_10.12_spmd, %region_13.13_spmd} | conditional | flops 482547712 | bytes 14201888 | solution.py:134
  350.4 2.3 fusion.12
  357.6 5.2 %conditional.3 = (f32[1,7,256]{2,1,0:T(8,128)S(1)}, f32[1,7,256]{2,1,0:T(8,128)S(1)}, f32[1,7,256,128]{3,2,1,0:T(8,128)S(1)}) conditional(s32[]{:T(128)} %convert_element_type.127, (s32[]{:T(128)}, s32[]{:T(128)}, s32[256]{0:T(256)S(1)}, s32[1,512]{1,0:T(1,128)S(1)}, bf16[32,512,1,128]{3,1,2,0:T(8,128)(2,1)}, /*index=5*/s32[]{:T(128)}, ...), branch_computations={%region_10.12_spmd, %region_13.13_spmd} | conditional | flops 482547712 | bytes 14201888 | solution.py:134
  359.5 2.3 fusion.12
  366.7 5.2 %conditional.3 = (f32[1,7,256]{2,1,0:T(8,128)S(1)}, f32[1,7,256]{2,1,0:T(8,128)S(1)}, f32[1,7,256,128]{3,2,1,0:T(8,128)S(1)}) conditional(s32[]{:T(128)} %convert_element_type.127, (s32[]{:T(128)}, s32[]{:T(128)}, s32[256]{0:T(256)S(1)}, s32[1,512]{1,0:T(1,128)S(1)}, bf16[32,512,1,128]{3,1,2,0:T(8,128)(2,1)}, /*index=5*/s32[]{:T(128)}, ...), branch_computations={%region_10.12_spmd, %region_13.13_spmd} | conditional | flops 482547712 | bytes 14201888 | solution.py:134
  368.6 2.3 fusion.12
  375.8 5.2 %conditional.3 = (f32[1,7,256]{2,1,0:T(8,128)S(1)}, f32[1,7,256]{2,1,0:T(8,128)S(1)}, f32[1,7,256,128]{3,2,1,0:T(8,128)S(1)}) conditional(s32[]{:T(128)} %convert_element_type.127, (s32[]{:T(128)}, s32[]{:T(128)}, s32[256]{0:T(256)S(1)}, s32[1,512]{1,0:T(1,128)S(1)}, bf16[32,512,1,128]{3,1,2,0:T(8,128)(2,1)}, /*index=5*/s32[]{:T(128)}, ...), branch_computations={%region_10.12_spmd, %region_13.13_spmd} | conditional | flops 482547712 | bytes 14201888 | solution.py:134
  377.6 2.3 fusion.12
  384.8 5.2 %conditional.3 = (f32[1,7,256]{2,1,0:T(8,128)S(1)}, f32[1,7,256]{2,1,0:T(8,128)S(1)}, f32[1,7,256,128]{3,2,1,0:T(8,128)S(1)}) conditional(s32[]{:T(128)} %convert_element_type.127, (s32[]{:T(128)}, s32[]{:T(128)}, s32[256]{0:T(256)S(1)}, s32[1,512]{1,0:T(1,128)S(1)}, bf16[32,512,1,128]{3,1,2,0:T(8,128)(2,1)}, /*index=5*/s32[]{:T(128)}, ...), branch_computations={%region_10.12_spmd, %region_13.13_spmd} | conditional | flops 482547712 | bytes 14201888 | solution.py:134
  386.7 2.3 fusion.12
  393.9 5.2 %conditional.3 = (f32[1,7,256]{2,1,0:T(8,128)S(1)}, f32[1,7,256]{2,1,0:T(8,128)S(1)}, f32[1,7,256,128]{3,2,1,0:T(8,128)S(1)}) conditional(s32[]{:T(128)} %convert_element_type.127, (s32[]{:T(128)}, s32[]{:T(128)}, s32[256]{0:T(256)S(1)}, s32[1,512]{1,0:T(1,128)S(1)}, bf16[32,512,1,128]{3,1,2,0:T(8,128)(2,1)}, /*index=5*/s32[]{:T(128)}, ...), branch_computations={%region_10.12_spmd, %region_13.13_spmd} | conditional | flops 482547712 | bytes 14201888 | solution.py:134
  395.8 2.3 fusion.12
  403.0 5.2 %conditional.3 = (f32[1,7,256]{2,1,0:T(8,128)S(1)}, f32[1,7,256]{2,1,0:T(8,128)S(1)}, f32[1,7,256,128]{3,2,1,0:T(8,128)S(1)}) conditional(s32[]{:T(128)} %convert_element_type.127, (s32[]{:T(128)}, s32[]{:T(128)}, s32[256]{0:T(256)S(1)}, s32[1,512]{1,0:T(1,128)S(1)}, bf16[32,512,1,128]{3,1,2,0:T(8,128)(2,1)}, /*index=5*/s32[]{:T(128)}, ...), branch_computations={%region_10.12_spmd, %region_13.13_spmd} | conditional | flops 482547712 | bytes 14201888 | solution.py:134
  404.9 2.3 fusion.12
  (378 shorter events, 115.7 us)
Async XLA Ops:
  7.2 1.7 copy-start.1
  7.2 1.0 copy-start.2
  7.2 1.0 copy-start.5
  7.2 0.9 copy-start.4
  7.2 83.3 %all-gather.5.cloned.1.call-start = ((), (), s32[]{:S(2)}) async-start(), calls=%async_computation.4 | async-start | bytes 8386560 | tf_op jit(solution)/shard_map/all_gather | solution.py:29
  21.9 5.2 %copy-start.7 = (s32[64]{0:T(128)S(1)}, s32[64]{0:T(128)}, u32[]{:S(2)}) copy-start(s32[64]{0:T(128)} %param.18) | copy-start | bytes 772
  23.4 6.4 %all-to-all-start.1 = ((f32[2,64,3584]{2,1,0:T(8,128)}), f32[2,64,3584]{2,1,0:T(8,128)S(1)}, u32[]{:S(2)}, u32[]{:S(2)}) async-start(f32[2,64,3584]{2,1,0:T(8,128)} %broadcast_in_dim.137), calls=%async_computation.1 | async-start | bytes 3670016 | tf_op jit(solution)/shard_map/all_to_all | solution.py:15
  29.8 16.5 %all-to-all-start = ((s32[64,1,2]{2,1,0:T(1,128)}), s32[64,1,2]{2,1,0:T(1,128)S(1)}, u32[]{:S(2)}, u32[]{:S(2)}) async-start(s32[64,1,2]{2,1,0:T(1,128)} %bitcast.14), calls=%async_computation | async-start | bytes 65536 | tf_op jit(solution)/shard_map/all_to_all | solution.py:110
  40.4 15.1 %copy-start.6 = (s32[3,256]{1,0:T(4,128)S(1)}, s32[3,256]{1,0:T(4,128)}, u32[]{:S(2)}) copy-start(s32[3,256]{1,0:T(4,128)} %param.21) | copy-start | bytes 9220
  41.5 28.1 %copy-start = (bf16[256,3584]{1,0:T(8,128)(2,1)S(1)}, bf16[256,3584]{1,0:T(8,128)(2,1)}, u32[]{:S(2)}) copy-start(bf16[256,3584]{1,0:T(8,128)(2,1)} %param.20) | copy-start | bytes 5505028
  46.4 22.0 %all-to-all-start.2 = ((bf16[64,2,3584]{2,1,0:T(2,128)(2,1)}), bf16[64,2,3584]{2,1,0:T(2,128)(2,1)S(1)}, u32[]{:S(2)}, u32[]{:S(2)}) async-start(bf16[64,2,3584]{2,1,0:T(2,128)(2,1)} %reshape.562), calls=%async_computation.2 | async-start | bytes 1835008 | tf_op jit(solution)/shard_map/all_to_all | solution.py:109
  55.4 112.9 %all-gather.7.cloned.1.call-start = ((), (), s32[]{:S(2)}) async-start(), calls=%async_computation.5 | async-start | bytes 4259840 | tf_op jit(solution)/shard_map/all_gather | solution.py:156
  73.8 22.3 %copy-start.3 = (s32[256]{0:T(256)S(1)}, s32[256]{0:T(256)}, u32[]{:S(2)}) copy-start(s32[256]{0:T(256)} %param.22) | copy-start | bytes 3076
  93.5 144.4 %all-gather.9.cloned.1.call-start = ((), (), s32[]{:S(2)}) async-start(), calls=%async_computation.6 | async-start | bytes 4259840 | tf_op jit(solution)/shard_map/all_gather | solution.py:157
  96.8 15.6 %all-to-all-start.3 = ((s32[64,256,1]{1,2,0:T(1,128)}), s32[64,256,1]{1,2,0:T(1,128)S(1)}, u32[]{:S(2)}, u32[]{:S(2)}) async-start(s32[64,256,1]{1,2,0:T(1,128)} %all_to_all.22), calls=%async_computation.3 | async-start | bytes 131072 | tf_op jit(solution)/shard_map/all_to_all | solution.py:160
Sparse Core Ops, SparseCore 0:
  11.5 78.9 all-gather.4
  93.7 74.6 all-gather.6
  171.3 66.6 all-gather.8
